TPU v7x, 32 devices: a whole 2x2x4 slice. The times are simulated.
32 devices in a mesh: dp: 32 (over z, y, x, core).
Axes of the slice: x: 2, y: 2, z: 4, core: 2. Of those that a mesh axis runs over, the one named last changes fastest.
Arguments:
- captions: bfloat16 [1024, 77, 768], P('dp'), may hold values from -6 to 6
- caption_layout: int32 [2, 1024], replicated, may hold values from 0 to 77, as said below
- images: bfloat16 [1024, 768], P('dp'), may hold values from -0.24 to 0.24
- w_query: bfloat16 [768, 768], replicated, may hold values from -0.21875 to 0.21875
- w_keyval: bfloat16 [768, 1536], replicated, may hold values from -0.21875 to 0.21875
- w_out: bfloat16 [768, 768], replicated, may hold values from -0.21875 to 0.21875
- w_up: bfloat16 [768, 3072], replicated, may hold values from -0.21875 to 0.21875
- w_down: bfloat16 [3072, 768], replicated, may hold values from -0.109375 to 0.109375
- w_proj: bfloat16 [768, 768], replicated, may hold values from -0.009114583 to 0.009114583
Outputs:
- image_grad: float32 [1024, 768], P('dp')
- text_grad: float32 [1024, 768], P('dp')
Inputs may be any that keep to these rules, and one draw needn't show every extreme that they name: `caption_layout`: row 0 holds each caption's token count; row 1 is 1 where the caption is encoded by the next index of dp (index 0 after the last) and 0 where by its own. Exactly 8 of each device's captions carry 1. The captions one device encodes (its own that carry 0 and those carrying 1 of the index before it) hold at most 2048 tokens together, exactly that many on some device.
All inputs are finite; a program needn't handle non-finite values.
Results may differ from a plain program's by a relative error of at most 0.018.
Values may be sent and summed in bfloat16 or wider, within the bound.
A program may use at most 128 MiB of HBM per device.

v0:
```python
import math

import jax
import jax.numpy as jnp
from jax import lax
from jax.sharding import PartitionSpec as P

HEADS = 12
HAND = 8
TOK_CAP = 2048


LOGIT_SCALE = 100.0
EPS_NORM = 1e-05
EPS_UNIT = 1e-06


def from_behind(value, axis, steps):
    count = lax.axis_size(axis)
    pairs = [(source, (source + steps) % count) for source in range(count)]
    return lax.ppermute(value, axis, pairs)


def layer_norm(values):
    values = values.astype(jnp.float32)
    center = values - jnp.mean(values, axis=-1, keepdims=True)
    spread = jnp.mean(center * center, axis=-1, keepdims=True)
    return center * lax.rsqrt(spread + EPS_NORM)


def unit_rows(values):
    values = values.astype(jnp.float32)
    return values * lax.rsqrt(jnp.sum(values * values, axis=-1, keepdims=True) + EPS_UNIT)


def contract_first(left, right):
    return lax.dot_general(
        left, right, (((0,), (0,)), ((), ())), preferred_element_type=jnp.float32
    )


def contract_last(left, right):
    return lax.dot_general(
        left, right, (((1,), (1,)), ((), ())), preferred_element_type=jnp.float32
    )


def encode(token_rows, slot_starts, slot_lengths, weight_set):
    w_query, w_keyval, w_out, w_up, w_down, w_proj = weight_set
    total_rows, model_width = token_rows.shape
    head_dim = model_width // HEADS
    normed = layer_norm(token_rows).astype(jnp.bfloat16)
    keyval = jnp.dot(normed, w_keyval, preferred_element_type=jnp.float32).astype(jnp.bfloat16)
    last_row = jnp.clip(slot_starts + slot_lengths - 1, 0, total_rows - 1)
    query = jnp.dot(normed[last_row], w_query, preferred_element_type=jnp.float32).astype(
        jnp.bfloat16
    )
    key_heads = keyval[:, :model_width].reshape(total_rows, HEADS, head_dim)
    value_heads = keyval[:, model_width:].reshape(total_rows, HEADS, head_dim)
    query_heads = query.reshape(-1, HEADS, head_dim)
    scores = jnp.einsum("shd,rhd->hsr", query_heads, key_heads, preferred_element_type=jnp.float32)
    scores = scores / math.sqrt(head_dim)
    position = jnp.arange(total_rows)[None, :]
    inside = (position >= slot_starts[:, None]) & (position < (slot_starts + slot_lengths)[:, None])
    inside = jnp.where(slot_lengths[:, None] > 0, inside, position == 0)
    masked = jnp.where(inside[None], scores, -jnp.inf)
    peak = jnp.max(masked, axis=-1, keepdims=True)
    exponent = jnp.exp(masked - peak)
    attention = (exponent / jnp.sum(exponent, axis=-1, keepdims=True)).astype(jnp.bfloat16)
    mixed_heads = jnp.einsum(
        "hsr,rhd->shd", attention, value_heads, preferred_element_type=jnp.float32
    )
    mixed_heads = mixed_heads.astype(jnp.bfloat16).reshape(-1, model_width)
    residual = token_rows[last_row].astype(jnp.float32) + jnp.dot(
        mixed_heads, w_out, preferred_element_type=jnp.float32
    )
    residual = residual.astype(jnp.bfloat16)
    inner_norm = layer_norm(residual).astype(jnp.bfloat16)
    hidden = jax.nn.gelu(
        jnp.dot(inner_norm, w_up, preferred_element_type=jnp.float32), approximate=False
    )
    hidden = hidden.astype(jnp.bfloat16)
    final_rows = residual.astype(jnp.float32) + jnp.dot(
        hidden, w_down, preferred_element_type=jnp.float32
    )
    pooled = layer_norm(final_rows).astype(jnp.bfloat16)
    return jnp.dot(pooled, w_proj, preferred_element_type=jnp.float32).astype(jnp.bfloat16)


def hand_slots(handed_flags, slot_total):
    before = jnp.cumsum(handed_flags) - handed_flags
    slot_index = jnp.arange(slot_total)[:, None]
    picked = (handed_flags[None, :] == 1) & (before[None, :] == slot_index)
    caption_index = jnp.arange(handed_flags.shape[0])[None, :]
    source = jnp.sum(jnp.where(picked, caption_index, 0), axis=1)
    return (before, source, jnp.any(picked, axis=1))


def body(captions, caption_layout, images, w_query, w_keyval, w_out, w_up, w_down, w_proj):
    caption_count, context, model_width = captions.shape
    device_count = lax.axis_size("dp")
    device_index = lax.axis_index("dp")
    weight_set = (w_query, w_keyval, w_out, w_up, w_down, w_proj)
    own_lengths = lax.dynamic_slice_in_dim(
        caption_layout[0], device_index * caption_count, caption_count
    )
    image_unit = unit_rows(images).astype(jnp.bfloat16)
    all_images = lax.all_gather(image_unit, "dp", axis=0, tiled=True)
    own_flags = lax.dynamic_slice_in_dim(
        caption_layout[1], device_index * caption_count, caption_count
    )
    previous = (device_index + device_count - 1) % device_count
    prev_lengths = lax.dynamic_slice_in_dim(
        caption_layout[0], previous * caption_count, caption_count
    )
    prev_flags = lax.dynamic_slice_in_dim(
        caption_layout[1], previous * caption_count, caption_count
    )
    before, source, slot_live = hand_slots(own_flags, HAND)
    outgoing = jnp.take(captions, source, axis=0)
    incoming = from_behind(outgoing, "dp", 1)
    prev_before, prev_source, prev_live = hand_slots(prev_flags, HAND)
    incoming_lengths = jnp.where(prev_live, prev_lengths[prev_source], 0)
    slot_lengths = jnp.concatenate([jnp.where(own_flags == 1, 0, own_lengths), incoming_lengths])
    slot_ends = jnp.cumsum(slot_lengths)
    slot_starts = slot_ends - slot_lengths
    position = jnp.arange(TOK_CAP)
    slot_of = jnp.sum((slot_ends[None, :] <= position[:, None]).astype(jnp.int32), axis=1)
    slot_of = jnp.minimum(slot_of, slot_lengths.shape[0] - 1)
    offset = jnp.clip(position - slot_starts[slot_of], 0, context - 1)
    stacked = jnp.concatenate([captions, incoming], axis=0).reshape(-1, model_width)
    token_rows = jnp.take(stacked, slot_of * context + offset, axis=0)
    encoded = encode(token_rows, slot_starts, slot_lengths, weight_set)
    returned = from_behind(encoded[caption_count:], "dp", -1)
    own_text = jnp.where(
        (own_flags == 1)[:, None], returned[jnp.clip(before, 0, HAND - 1)], encoded[:caption_count]
    )
    text_unit = unit_rows(own_text).astype(jnp.bfloat16)
    all_texts = lax.all_gather(text_unit, "dp", axis=0, tiled=True)
    row_scores = LOGIT_SCALE * contract_last(image_unit, all_texts)
    column_scores = LOGIT_SCALE * contract_last(all_images, text_unit)
    row_peak = jnp.max(row_scores, axis=1, keepdims=True)
    row_logsum = row_peak[:, 0] + jnp.log(jnp.sum(jnp.exp(row_scores - row_peak), axis=1))
    column_peak = jnp.max(column_scores, axis=0, keepdims=True)
    column_logsum = column_peak[0] + jnp.log(jnp.sum(jnp.exp(column_scores - column_peak), axis=0))
    row_weights = jnp.exp(row_scores - row_logsum[:, None]).astype(jnp.bfloat16)
    column_weights = jnp.exp(column_scores - column_logsum[None, :]).astype(jnp.bfloat16)
    half_scale = 0.5 * LOGIT_SCALE
    image_unit_grad = half_scale * jnp.dot(
        row_weights, all_texts, preferred_element_type=jnp.float32
    )
    image_unit_grad = image_unit_grad - LOGIT_SCALE * text_unit.astype(jnp.float32)
    text_unit_grad = half_scale * contract_first(column_weights, all_images)
    text_unit_grad = text_unit_grad - LOGIT_SCALE * image_unit.astype(jnp.float32)
    row_every, column_every = (
        lax.all_gather(row_logsum, "dp", axis=0, tiled=True),
        lax.all_gather(column_logsum, "dp", axis=0, tiled=True),
    )
    cross_rows = jnp.exp(row_scores - column_every[None, :]).astype(jnp.bfloat16)
    cross_columns = jnp.exp(column_scores - row_every[:, None]).astype(jnp.bfloat16)
    image_unit_grad = image_unit_grad + half_scale * jnp.dot(
        cross_rows, all_texts, preferred_element_type=jnp.float32
    )
    text_unit_grad = text_unit_grad + half_scale * contract_first(cross_columns, all_images)
    image_value, image_back = jax.vjp(unit_rows, images.astype(jnp.float32))
    text_value, text_back = jax.vjp(unit_rows, own_text.astype(jnp.float32))
    return (image_back(image_unit_grad)[0], text_back(text_unit_grad)[0])


def solution(mesh):
    return jax.shard_map(
        body,
        mesh=mesh,
        in_specs=(P("dp", None, None), P(), P("dp", None), P(), P(), P(), P(), P(), P()),
        out_specs=(P("dp", None), P("dp", None)),
        check_vma=False,
    )
```

profile of v0, /device:TPU:0, one launch (start us, length us, event | category | flops | bytes accessed | tf_op | source)
XLA Modules:
  0.0 240.3 jit_solution(14694527201898477411)
XLA Ops:
  7.2 1.1 fusion.63
  8.3 0.6 copy-done.18
  8.9 0.5 copy-done.13
  9.4 1.5 fusion.64
  11.0 0.8 fusion.133
  12.1 0.7 fusion.87
  13.0 3.6 %gather_fusion.1 = bf16[8,77,768]{2,0,1:T(8,128)(2,1)S(1)} fusion(bf16[32,77,768]{2,0,1:T(8,128)(2,1)} %param.9, s32[1024]{0:T(1024)S(1)} %pad_clamp_fusion.2), kind=kCustom, calls=%fused_computation.1 | custom fusion | bytes 1892384 | tf_op jit(solution)/shard_map/jit(_take)/gather | solution.py:120
  16.5 1.1 broadcast_select_fusion.1
  17.6 0.5 collective-permute-start
  18.7 0.6 gather_fusion
  19.8 0.6 fusion.136
  20.4 0.7 fusion.135
  21.1 0.7 fusion.134
  21.9 4.4 %compare_select_fusion.4 = (s32[2048,1]{0,1:T(1,128)S(1)}, s32[2048,1]{0,1:T(1,128)S(1)}) fusion(s32[]{:T(128)} %bitcast.42, s32[]{:T(128)} %bitcast.43, s32[]{:T(128)} %bitcast.44, s32[]{:T(128)} %bitcast.45, s32[]{:T(128)} %bitcast.46, s32[]{:T(128)} %bitcast.48, s32[]{:T(128)} %bitcast.47, s32[2048,1]{0,1:T(1,128)S(1)} %bitcast.100), kind=kLoop, calls=%fused_computation.175 | loop fusion | flops 30720 | bytes 24604 | tf_op jit(solution)/shard_map/gather | solution.py:130
  26.3 0.8 compare_reduce_fusion.32
  27.1 20.6 %compare_and_fusion = (pred[2048]{0:T(1024)(128)(4,1)S(1)}, s32[2048]{0:T(1024)S(1)}) fusion(s32[2048]{0:T(1024)S(1)} %convert_reduce_fusion.1, pred[2048]{0:T(1024)(128)(4,1)S(1)} %get-tuple-element.38, pred[2048]{0:T(1024)(128)(4,1)S(1)} %get-tuple-element.37, pred[2048]{0:T(1024)(128)(4,1)S(1)} %get-tuple-element.36, ...), kind=kLoop, calls=%fused_computation.187 | loop fusion | flops 90112 | bytes 94340 | tf_op jit(solution)/shard_map/jit(_take)/and | solution.py:132
  47.8 0.8 fusion.29
  48.6 2.4 pad_maximum_fusion
  51.0 3.1 %copy.24 = bf16[40,77,768]{2,1,0:T(8,128)(2,1)} copy(bf16[40,77,768]{2,0,1:T(8,128)(2,1)S(1)} %pad_maximum_fusion) | data formatting | bytes 9461760 | tf_op jit(solution)/shard_map/concatenate | solution.py:131
  54.2 6.9 %reshape.374 = bf16[3080,768]{1,0:T(8,128)(2,1)} reshape(bf16[40,77,768]{2,1,0:T(8,128)(2,1)} %copy.24) | data formatting | bytes 9461760 | tf_op jit(solution)/shard_map/reshape | solution.py:131
  61.1 13.0 %gather_fusion.2 = bf16[2048,768]{1,0:T(8,128)(2,1)} fusion(bf16[3080,768]{1,0:T(8,128)(2,1)} %reshape.374, s32[2048]{0:T(1024)S(1)} %broadcast_clamp_fusion), kind=kCustom, calls=%fused_computation.2 | custom fusion | bytes 6299648 | tf_op jit(solution)/shard_map/jit(_take)/gather | solution.py:132
  74.1 2.6 %convert_reduce_fusion = (f32[2048]{0:T(1024)S(1)}, bf16[2048,768]{1,0:T(8,128)(2,1)S(1)}) fusion(bf16[2048,768]{1,0:T(8,128)(2,1)} %gather_fusion.2, pred[2048]{0:T(1024)(128)(4,1)S(1)} %get-tuple-element.51), kind=kLoop, calls=%fused_computation.8 | loop fusion | flops 4716544 | bytes 6301696 | tf_op jit(solution)/shard_map/reduce_sum | solution.py:26
  76.8 1.7 copy-done.2
  78.5 1.1 fusion.3
  79.6 3.6 %gather_fusion.3 = bf16[40,768]{1,0:T(8,128)(2,1)} fusion(bf16[2048,768]{1,0:T(8,128)(2,1)} %copy-done.2, s32[1024]{0:T(1024)S(1)} %pad_clamp_fusion.1), kind=kCustom, calls=%fused_computation.3 | custom fusion | bytes 123040 | tf_op jit(solution)/shard_map/gather | solution.py:74
  83.2 3.6 %fusion.4 = bf16[2048,768]{1,0:T(8,128)(2,1)} fusion(bf16[2048,768]{1,0:T(8,128)(2,1)} %copy-done.2, f32[2048]{0:T(1024)S(1)} %add_rsqrt_fusion, f32[2048]{0:T(1024)S(1)} %broadcast_multiply_fusion), kind=kLoop, calls=%fused_computation.13 | loop fusion | flops 6291456 | bytes 6307840 | tf_op jit(solution)/shard_map/convert_element_type | solution.py:52
  86.8 3.7 %gather_fusion.4 = bf16[40,768]{1,0:T(8,128)(2,1)} fusion(bf16[2048,768]{1,0:T(8,128)(2,1)} %fusion.4, s32[1024]{0:T(1024)} %copy-done.12), kind=kCustom, calls=%fused_computation.4 | custom fusion | bytes 123040 | tf_op jit(solution)/shard_map/gather | solution.py:55
  90.5 1.8 convolution_convert_fusion.2
  92.3 1.0 reshape.376
  93.3 7.5 %convolution_convert_fusion = bf16[2048,1536]{0,1:T(8,128)(2,1)S(1)} fusion(bf16[2048,768]{1,0:T(8,128)(2,1)} %fusion.4, bf16[768,1536]{1,0:T(8,128)(2,1)S(1)} %copy-done), kind=kOutput, calls=%fused_computation.9 | convolution fusion | flops 4834983936 | bytes 11796480 | tf_op jit(solution)/shard_map/dot_general | solution.py:53
  100.8 3.2 %fusion.132 = (bf16[2048,768]{0,1:T(8,128)(2,1)}, bf16[2048,768]{0,1:T(8,128)(2,1)}) fusion(bf16[2048,1536]{0,1:T(8,128)(2,1)S(1)} %convolution_convert_fusion), kind=kLoop, calls=%fused_computation.268 | loop fusion | bytes 12582912 | tf_op jit(solution)/shard_map/slice | solution.py:58
  104.0 5.3 %fusion.137 = (f32[12,40]{1,0:T(8,128)S(1)}, f32[12,40,2048]{2,1,0:T(8,128)}) fusion(pred[40,2048]{1,0:T(8,128)(4,1)S(1)} %copy-done.11, bf16[2048,12,64]{0,2,1:T(8,128)(2,1)} %bitcast.99, bf16[40,12,64]{2,1,0:T(8,128)(2,1)S(1)} %reshape.376), kind=kOutput, calls=%fused_computation.273 | convolution fusion | flops 129763328 | bytes 7223168 | tf_op jit(solution)/shard_map/sub | solution.py:68
  109.3 4.2 %fusion.11 = bf16[40,12,64]{2,0,1:T(8,128)(2,1)S(1)} fusion(bf16[2048,12,64]{0,2,1:T(8,128)(2,1)} %bitcast.98, f32[12,40,2048]{2,1,0:T(8,128)} %get-tuple-element.103, f32[12,40]{1,0:T(8,128)S(1)} %get-tuple-element.102), kind=kOutput, calls=%fused_computation.27 | convolution fusion | flops 127825920 | bytes 7141248 | tf_op jit(solution)/shard_map/hsr,rhd->shd/dot_general | solution.py:70
  114.4 6.3 %fusion.141 = (f32[40]{0:T(128)S(1)}, f32[40,768]{1,0:T(8,128)S(1)}) fusion(f32[40,768]{1,0:T(8,128)S(1)} %get-tuple-element.105, bf16[3072,768]{1,0:T(8,128)(2,1)} %param.16, bf16[768,3072]{1,0:T(8,128)(2,1)} %param.15, f32[40]{0:T(128)S(1)} %add_rsqrt_fusion.2, f32[40]{0:T(128)S(1)} %broadcast_multiply_fusion.2), kind=kOutput, calls=%fused_computation.275 | convolution fusion | flops 385628128 | bytes 9683424 | tf_op jit(solution)/shard_map/dot_general | solution.py:83
  121.3 6.0 %collective-permute-start.1 = (bf16[8,768]{1,0:T(8,128)(2,1)S(1)}, bf16[8,768]{1,0:T(8,128)(2,1)S(1)}, u32[]{:S(2)}, u32[]{:S(2)}) collective-permute-start(bf16[8,768]{1,0:T(8,128)(2,1)S(1)} %slice.81), channel_id=1, source_target_pairs={{0,31},{1,0},{2,1},{3,2},{4,3},{5,4},{6,5},{7,6},{8,7},{9,8},{10,9... | collective-permute-start | bytes 36872 | tf_op jit(solution)/shard_map/ppermute | solution.py:21
  127.3 1.4 collective-permute-done.1
  128.7 0.6 gather_fusion.5
  129.5 0.7 fusion.67
  130.3 2.1 fusion.143
  132.7 1.8 fusion.13
  134.6 51.8 %all-gather.3.cloned.1.call-done = bf16[1024,768]{1,0:T(8,128)(2,1)} async-done(((bf16[32,768]{1,0:T(8,128)(2,1)}), bf16[1024,768]{1,0:T(8,128)(2,1)}) %all-gather.3.cloned.1.call-update) | async-done | bytes 1572880 | tf_op jit(solution)/shard_map/all_gather | solution.py:139
  186.4 2.1 fusion.142
  188.8 38.9 %all-reduce.2 = (f32[1024]{0:T(1024)S(1)}, f32[1024]{0:T(1024)S(1)}) all-reduce(f32[1024]{0:T(1024)S(1)} %get-tuple-element.43, f32[1024]{0:T(1024)S(1)} %get-tuple-element.41), channel_id=1, replica_groups=mesh['dp'=32] {'dp'}, use_global_device_ids=true, to_apply=%add | all-reduce | flops 2048 | bytes 16384
  227.7 1.9 fusion.15
  229.6 1.9 fusion.65
  231.6 0.5 fusion.68
  232.1 0.7 add_add_fusion.1
  232.8 0.7 add_add_fusion
  (96 shorter events, 4.1 us)
Async XLA Ops:
  7.2 86.1 %copy-start = (bf16[768,1536]{1,0:T(8,128)(2,1)S(1)}, bf16[768,1536]{1,0:T(8,128)(2,1)}, u32[]{:S(2)}) copy-start(bf16[768,1536]{1,0:T(8,128)(2,1)} %param.13) | copy-start | bytes 7077892
  7.2 123.1 %all-gather.5.cloned.1.call-start = ((), (), s32[]{:S(2)}) async-start(), calls=%async_computation.1 | async-start | bytes 1622016 | tf_op jit(solution)/shard_map/all_gather | solution.py:108
  8.3 0.6 copy-start.18
  8.9 0.5 copy-start.13
  10.9 175.5 %all-gather.3.cloned.1.call-start = ((), (), s32[]{:S(2)}) async-start(), calls=%async_computation | async-start | bytes 1622016 | tf_op jit(solution)/shard_map/all_gather | solution.py:139
  11.9 1.0 copy-start.15
  17.6 31.0 %collective-permute-start = (bf16[8,77,768]{2,0,1:T(8,128)(2,1)}, bf16[8,77,768]{2,0,1:T(8,128)(2,1)S(1)}, u32[]{:S(2)}, u32[]{:S(2)}) collective-permute-start(bf16[8,77,768]{2,0,1:T(8,128)(2,1)} %broadcast_select_fusion.1), channel_id=1, source_target_pairs={{0,1},{1,2},{2,3},{3,4},{4,5},{5,6},{6,7},{7,8},{8,9},{9,10},{10,1... | collective-permute-start | bytes 2838536 | tf_op jit(solution)/shard_map/ppermute | solution.py:21
  47.8 31.8 %copy-start.12 = (s32[1024]{0:T(1024)}, s32[1024]{0:T(1024)S(1)}, u32[]{:S(2)}) copy-start(s32[1024]{0:T(1024)S(1)} %pad_clamp_fusion.1) | copy-start | bytes 12292
  76.8 1.7 copy-start.2
  83.2 7.3 %copy-start.4 = (bf16[768,768]{1,0:T(8,128)(2,1)S(1)}, bf16[768,768]{1,0:T(8,128)(2,1)}, u32[]{:S(2)}) copy-start(bf16[768,768]{1,0:T(8,128)(2,1)} %param.12) | copy-start | bytes 3538948
  100.8 3.2 %copy-start.11 = (pred[40,2048]{1,0:T(8,128)(4,1)S(1)}, pred[40,2048]{1,0:T(8,128)(4,1)}, u32[]{:S(2)}) copy-start(pred[40,2048]{1,0:T(8,128)(4,1)} %fusion.29) | copy-start | bytes 245764
  109.3 4.4 %copy-start.6 = (bf16[768,768]{1,0:T(8,128)(2,1)S(1)}, bf16[768,768]{1,0:T(8,128)(2,1)}, u32[]{:S(2)}) copy-start(bf16[768,768]{1,0:T(8,128)(2,1)} %param.14) | copy-start | bytes 3538948
  109.3 4.4 %copy-start.10 = (bf16[40,768]{1,0:T(8,128)(2,1)S(1)}, bf16[40,768]{1,0:T(8,128)(2,1)}, u32[]{:S(2)}) copy-start(bf16[40,768]{1,0:T(8,128)(2,1)} %gather_fusion.3) | copy-start | bytes 184324
  114.3 6.6 %copy-start.5 = (bf16[768,768]{1,0:T(8,128)(2,1)S(1)}, bf16[768,768]{1,0:T(8,128)(2,1)}, u32[]{:S(2)}) copy-start(bf16[768,768]{1,0:T(8,128)(2,1)} %param.17) | copy-start | bytes 3538948
  114.3 12.9 %copy-start.17 = (s32[32]{0:T(128)S(1)}, s32[32]{0:T(128)}, u32[]{:S(2)}) copy-start(s32[32]{0:T(128)} %get-tuple-element.4) | copy-start | bytes 388
  114.4 15.0 %copy-start.16 = (pred[32]{0:T(512)(128)(4,1)S(1)}, pred[32]{0:T(512)(128)(4,1)}, u32[]{:S(2)}) copy-start(pred[32]{0:T(512)(128)(4,1)} %copy-done.15) | copy-start | bytes 100
  120.7 12.0 %copy-start.7 = (bf16[32,768]{1,0:T(8,128)(2,1)S(1)}, bf16[32,768]{1,0:T(8,128)(2,1)}, u32[]{:S(2)}) copy-start(bf16[32,768]{1,0:T(8,128)(2,1)} %fusion.64) | copy-start | bytes 147460
  121.3 7.4 %collective-permute-start.1 = (bf16[8,768]{1,0:T(8,128)(2,1)S(1)}, bf16[8,768]{1,0:T(8,128)(2,1)S(1)}, u32[]{:S(2)}, u32[]{:S(2)}) collective-permute-start(bf16[8,768]{1,0:T(8,128)(2,1)S(1)} %slice.81), channel_id=1, source_target_pairs={{0,31},{1,0},{2,1},{3,2},{4,3},{5,4},{6,5},{7,6},{8,7},{9,8},{10,9... | collective-permute-start | bytes 36872 | tf_op jit(solution)/shard_map/ppermute | solution.py:21
  130.2 97.4 %copy-start.8 = (bf16[32,768]{1,0:T(8,128)(2,1)S(1)}, bf16[32,768]{1,0:T(8,128)(2,1)}, u32[]{:S(2)}) copy-start(bf16[32,768]{1,0:T(8,128)(2,1)} %fusion.67) | copy-start | bytes 147460
  132.4 97.2 %copy-start.9 = (bf16[32,768]{1,0:T(8,128)(2,1)S(1)}, bf16[32,768]{1,0:T(8,128)(2,1)}, u32[]{:S(2)}) copy-start(bf16[32,768]{1,0:T(8,128)(2,1)} %param.11) | copy-start | bytes 147460
  134.6 96.9 %copy-start.19 = (f32[32]{0:T(128)S(1)}, f32[32]{0:T(128)}, u32[]{:S(2)}) copy-start(f32[32]{0:T(128)} %copy-done.18) | copy-start | bytes 388
  188.5 43.6 %copy-start.14 = (f32[32]{0:T(128)S(1)}, f32[32]{0:T(128)}, u32[]{:S(2)}) copy-start(f32[32]{0:T(128)} %copy-done.13) | copy-start | bytes 388
  188.5 45.0 %copy-start.1 = (bf16[768,1536]{1,0:T(8,128)(2,1)S(1)}, bf16[768,1536]{1,0:T(8,128)(2,1)}, u32[]{:S(2)}) copy-start(bf16[768,1536]{1,0:T(8,128)(2,1)} %param.13) | copy-start | bytes 7077892
  227.7 3.9 %copy-start.3 = (bf16[1024,768]{1,0:T(8,128)(2,1)S(1)}, bf16[1024,768]{1,0:T(8,128)(2,1)}, u32[]{:S(2)}) copy-start(bf16[1024,768]{1,0:T(8,128)(2,1)} %all-gather.5.cloned.1.call-done) | copy-start | bytes 4718596
Sparse Core Ops, SparseCore 0:
  11.0 59.7 all-gather.4
  130.4 55.9 all-gather.2
where the time goes:
time: 242 us; the launch traced here: 240 us
  waiting for transfers between devices  53.2 us (22%)
  local copies, waits for them, and re-layouts  45.6 us (19%)
  other arithmetic  45.4 us (19%)
  blocking collectives  38.9 us (16%)
  matrix products  36.2 us (15%)
  between operations  14.5 us (6%)
  starting transfers between devices  6.53 us (3%)
    all_gather x1, waiting for transfers between devices, body(): all_texts = lax.all_gather(text_unit, 'dp', axis=0, tiled=True)  51.8 us
    unnamed x1, blocking collectives  38.9 us
    and x1, other arithmetic, body(): token_rows = jnp.take(stacked, slot_of * context + offset, axis=0)  20.6 us
    gather x1, local copies, waits for them, and re-layouts, body(): token_rows = jnp.take(stacked, slot_of * context + offset, axis=0)  13 us
    dot_general x1, matrix products, encode(): jnp.dot(normed, w_keyval, preferred_element_type=jnp.float32)  7.47 us
    reshape x1, local copies, waits for them, and re-layouts, body(): jnp.concatenate([captions, incoming], axis=0).reshape(-1, model_width)  6.92 us
    ppermute x2, starting transfers between devices, from_behind(): return lax.ppermute(value, axis, pairs)  6.45 us
    dot_general x1, matrix products, encode(): jnp.dot(hidden, w_down, preferred_element_type=jnp.float32)  6.34 us
  transfers between devices with their start and end apart: 4, of which 2 were waited for; matrix products, arithmetic and copies ran while one was open for 47% of the time, Pallas kernels for 0%

commit v1 on v0

v1 whole, which is shorter than its diff:
```python
import functools

import jax
import jax.numpy as jnp
from jax import lax
from jax.experimental import pallas as pl
from jax.experimental.pallas import tpu as pltpu
from jax.sharding import PartitionSpec as P

HEADS = 12
LOGIT_SCALE = 100.0
EPS_NORM = 1e-05
EPS_UNIT = 1e-06
GROUP = 8
QUAD = 4
LSE_BLOCK = 256
FF_CHUNKS = 4
MESH = pl.DeviceIdType.MESH
F32 = jnp.float32
BF16 = jnp.bfloat16


def dot(a, b):
    return jnp.dot(a, b, preferred_element_type=F32)


def dot_last(a, b):
    return lax.dot_general(a, b, (((1,), (1,)), ((), ())), preferred_element_type=F32)


def dot_first(a, b):
    return lax.dot_general(a, b, (((0,), (0,)), ((), ())), preferred_element_type=F32)


def layer_norm(x):
    center = x - jnp.mean(x, axis=-1, keepdims=True)
    spread = jnp.mean(center * center, axis=-1, keepdims=True)
    return center * lax.rsqrt(spread + EPS_NORM)


def unit_rows(x):
    return x * lax.rsqrt(jnp.sum(x * x, axis=-1, keepdims=True) + EPS_UNIT)


def unit_back(x, g):
    s = jnp.sum(x * x, axis=-1, keepdims=True) + EPS_UNIT
    r = lax.rsqrt(s)
    return g * r - x * (jnp.sum(x * g, axis=-1, keepdims=True) * (r / s))


def kernel(
    n,
    cap_hbm, layout, images, wq_hbm, wkv_hbm, wo_hbm, wup_hbm, wdown_hbm, wproj_hbm,
    image_out, text_out,
    cap, normed, x_last, qk, mix, wq, wkv, wo, wup, wdown, wproj,
    gi, gt, row_lse, col_lse,
    load_sem, i_send, i_recv, i_rsend, i_rrecv, t_send, t_recv, t_rsend, t_rrecv,
):
    me = lax.axis_index("dp")
    half = n // 2
    partner = me + 1 - 2 * lax.rem(me, 2)
    caps, ctx, width = cap.shape
    groups = caps // GROUP
    slot = normed.shape[0] // caps
    head_dim = width // HEADS
    ff = wup.shape[1]
    fc = ff // FF_CHUNKS

    loads = []

    def load(src, dst):
        copy = pltpu.make_async_copy(src, dst, load_sem.at[len(loads)])
        copy.start()
        loads.append(copy)
        return copy

    cap_loads = [
        load(cap_hbm.at[pl.ds(g * GROUP, GROUP)], cap.at[pl.ds(g * GROUP, GROUP)])
        for g in range(groups)
    ]
    wq_load = load(wq_hbm, wq)
    wkv_load = load(wkv_hbm, wkv)
    wo_load = load(wo_hbm, wo)
    ff_loads = []
    for f in range(FF_CHUNKS):
        cols = pl.ds(f * fc, fc)
        ff_loads.append(
            (load(wup_hbm.at[:, cols], wup.at[:, cols]), load(wdown_hbm.at[cols], wdown.at[cols]))
        )
    wproj_load = load(wproj_hbm, wproj)

    barrier = pltpu.get_barrier_semaphore()

    def greet(k, carry):
        pl.semaphore_signal(
            barrier, inc=1, device_id=(lax.rem(me + 2 * k, n),), device_id_type=MESH
        )
        return carry

    lax.fori_loop(1, half, greet, 0)
    pl.semaphore_signal(barrier, inc=1, device_id=(partner,), device_id_type=MESH)

    def remote(buf, block, send, recv, target):
        return pltpu.make_async_remote_copy(
            src_ref=buf.at[block], dst_ref=buf.at[block], send_sem=send, recv_sem=recv,
            device_id=(target,), device_id_type=MESH,
        )

    def push(buf, send, recv, rsend, rrecv):
        def step(k, carry):
            remote(buf, me, send.at[k], recv.at[k], lax.rem(me + 2 * k, n)).start()
            return carry

        lax.fori_loop(1, half, step, 0)
        remote(buf, me, rsend.at[0], rrecv.at[0], partner).start()

    def relay(buf, send, recv, rsend, rrecv):
        def step(k, carry):
            block = lax.rem(me + n - 2 * k, n)
            remote(buf, block, send.at[k], recv.at[k], partner).wait_recv()
            remote(buf, block, rsend.at[k], rrecv.at[k], partner).start()
            return carry

        lax.fori_loop(1, half, step, 0)

    def finish(buf, send, recv, rsend, rrecv):
        def step(k, carry):
            block = lax.rem(partner + n - 2 * k, n)
            remote(buf, block, rsend.at[k], rrecv.at[k], partner).wait_recv()
            return carry

        lax.fori_loop(0, half, step, 0)

    def drain(buf, send, recv, rsend, rrecv):
        def step(k, carry):
            block = lax.rem(me + n - 2 * k, n)
            remote(buf, me, send.at[k], recv.at[k], partner).wait_send()
            remote(buf, block, rsend.at[k], rrecv.at[k], partner).wait_send()
            return carry

        lax.fori_loop(1, half, step, 0)
        remote(buf, me, rsend.at[0], rrecv.at[0], partner).wait_send()

    i_set = (gi, i_send, i_recv, i_rsend, i_rrecv)
    t_set = (gt, t_send, t_recv, t_rsend, t_rrecv)

    image = images[...].astype(F32)
    image_unit = unit_rows(image).astype(BF16)
    gi[me] = image_unit
    pl.semaphore_wait(barrier, half)
    push(*i_set)

    token = lax.broadcasted_iota(jnp.int32, (ctx, width), 0)
    tail = (ctx // 16) * 16
    for g in range(groups):
        cap_loads[g].wait()

        def norm_one(i, carry, g=g):
            c = g * GROUP + i
            x = cap[c].astype(F32)
            length = layout[0, me * caps + c]
            x_last[pl.ds(c, 1), :] = jnp.sum(
                jnp.where(token == length - 1, x, 0.0), axis=0, keepdims=True
            )
            base = pl.multiple_of(c * slot, 16)
            y = layer_norm(x).astype(BF16)
            normed[pl.ds(base, tail), :] = y[:tail]
            rest = jnp.concatenate(
                [y[tail:].astype(F32), jnp.zeros((slot - ctx, width), F32)], axis=0
            )
            normed[pl.ds(pl.multiple_of(base + tail, 16), slot - tail), :] = rest.astype(BF16)
            return carry

        lax.fori_loop(0, GROUP, norm_one, 0)

    last = x_last[...]
    last_normed = layer_norm(last).astype(BF16)
    wq_load.wait()
    query = dot(last_normed, wq[...]).astype(BF16).astype(F32) * (head_dim ** -0.5)
    wkv_load.wait()
    span = QUAD * head_dim
    lane = lax.broadcasted_iota(jnp.int32, (caps, span), 1)
    for b in range(HEADS // QUAD):
        piece = query[:, b * span : (b + 1) * span]
        stacked = jnp.concatenate(
            [
                jnp.where((lane >= j * head_dim) & (lane < (j + 1) * head_dim), piece, 0.0)
                for j in range(QUAD)
            ],
            axis=0,
        ).astype(BF16)
        part = dot_last(stacked, wkv[:, b * span : (b + 1) * span])
        qk[b * QUAD : (b + 1) * QUAD] = part.reshape(QUAD, caps, width)

    cols = HEADS * GROUP
    col_cap = lax.rem(lax.broadcasted_iota(jnp.int32, (1, cols), 1), GROUP)

    def attend(g, carry):
        base = pl.multiple_of(g * (GROUP * slot), 16)
        rows = normed[pl.ds(base, GROUP * slot), :]
        first = pl.multiple_of(g * GROUP, GROUP)
        keys = qk[:, pl.ds(first, GROUP), :].reshape(cols, width).astype(BF16)
        scores = dot_last(rows, keys)
        lengths = jnp.zeros((1, cols), jnp.int32)
        for i in range(GROUP):
            lengths = jnp.where(col_cap == i, layout[0, me * caps + g * GROUP + i], lengths)
        place = lax.broadcasted_iota(jnp.int32, scores.shape, 0) - col_cap * slot
        inside = (place >= 0) & (place < lengths)
        scores = jnp.where(inside, scores, -1e30)
        peak = jnp.max(scores, axis=0, keepdims=True)
        expo = jnp.where(inside, jnp.exp(scores - peak), 0.0)
        attn = (expo / jnp.sum(expo, axis=0, keepdims=True)).astype(BF16)
        mix[:, pl.ds(first, GROUP), :] = dot_first(attn, rows).reshape(HEADS, GROUP, width)
        return carry

    lax.fori_loop(0, groups, attend, 0)

    pieces = []
    for b in range(HEADS // QUAD):
        left = mix[b * QUAD : (b + 1) * QUAD].reshape(QUAD * caps, width).astype(BF16)
        wide = dot(left, wkv[:, width + b * span : width + (b + 1) * span])
        piece = wide[:caps]
        for j in range(1, QUAD):
            piece = jnp.where(lane >= j * head_dim, wide[j * caps : (j + 1) * caps], piece)
        pieces.append(piece)
    mixed = jnp.concatenate(pieces, axis=1).astype(BF16)
    wo_load.wait()
    residual = (last + dot(mixed, wo[...])).astype(BF16).astype(F32)
    inner = layer_norm(residual).astype(BF16)

    relay(*i_set)

    final = residual
    for f in range(FF_CHUNKS):
        up_load, down_load = ff_loads[f]
        up_load.wait()
        up = dot(inner, wup[:, f * fc : (f + 1) * fc])
        hidden = (0.5 * up * (1.0 + lax.erf(up * (2.0 ** -0.5)))).astype(BF16)
        down_load.wait()
        final = final + dot(hidden, wdown[f * fc : (f + 1) * fc])
    pooled = layer_norm(final).astype(BF16)
    wproj_load.wait()
    text = dot(pooled, wproj[...]).astype(BF16).astype(F32)
    text_unit = unit_rows(text).astype(BF16)
    gt[me] = text_unit
    push(*t_set)
    finish(*i_set)
    relay(*t_set)
    finish(*t_set)

    pairs = gi.shape[0] * gi.shape[1]
    step_blocks = LSE_BLOCK // caps

    def lse_block(b, carry):
        where = pl.ds(pl.multiple_of(b * LSE_BLOCK, LSE_BLOCK), LSE_BLOCK)
        for big, small, out in ((gi, gt, col_lse), (gt, gi, row_lse)):
            all_rows = big[...].reshape(pairs, width)
            block = small[pl.ds(b * step_blocks, step_blocks)].reshape(LSE_BLOCK, width)
            s = LOGIT_SCALE * dot_last(all_rows, block)
            peak = jnp.max(s, axis=0, keepdims=True)
            out[:, where] = peak + jnp.log(jnp.sum(jnp.exp(s - peak), axis=0, keepdims=True))
        return carry

    lax.fori_loop(0, pairs // LSE_BLOCK, lse_block, 0)

    half_scale = 0.5 * LOGIT_SCALE

    def grads(mine, others, other_lse, opposite):
        every = others[...].reshape(pairs, width)
        s = LOGIT_SCALE * dot_last(mine, every)
        peak = jnp.max(s, axis=1, keepdims=True)
        own = peak + jnp.log(jnp.sum(jnp.exp(s - peak), axis=1, keepdims=True))
        weights = jnp.concatenate(
            [jnp.exp(s - own), jnp.exp(s - other_lse)], axis=0
        ).astype(BF16)
        both = dot(weights, every)
        total = both[:caps] + both[caps:]
        return half_scale * total - LOGIT_SCALE * opposite.astype(F32)

    image_out[...] = unit_back(image, grads(image_unit, gt, col_lse[...], text_unit))
    text_out[...] = unit_back(text, grads(text_unit, gi, row_lse[...], image_unit))
    drain(*i_set)
    drain(*t_set)


def body(captions, caption_layout, images, w_query, w_keyval, w_out, w_up, w_down, w_proj):
    caps, ctx, width = captions.shape
    n = lax.axis_size("dp")
    slot = -(-ctx // 16) * 16
    half = n // 2
    pairs = n * caps
    loads = caps // GROUP + 4 + 2 * FF_CHUNKS
    any_spec = pl.BlockSpec(memory_space=pl.ANY)
    vmem = pl.BlockSpec(memory_space=pltpu.VMEM)
    smem = pl.BlockSpec(memory_space=pltpu.SMEM)
    out = jax.ShapeDtypeStruct(images.shape, F32)
    dma = pltpu.SemaphoreType.DMA
    return pl.pallas_call(
        functools.partial(kernel, n),
        out_shape=(out, out),
        in_specs=[any_spec, smem, vmem] + [any_spec] * 6,
        out_specs=(vmem, vmem),
        scratch_shapes=[
            pltpu.VMEM(captions.shape, BF16),
            pltpu.VMEM((caps * slot, width), BF16),
            pltpu.VMEM((caps, width), F32),
            pltpu.VMEM((HEADS, caps, width), F32),
            pltpu.VMEM((HEADS, caps, width), F32),
            pltpu.VMEM(w_query.shape, BF16),
            pltpu.VMEM(w_keyval.shape, BF16),
            pltpu.VMEM(w_out.shape, BF16),
            pltpu.VMEM(w_up.shape, BF16),
            pltpu.VMEM(w_down.shape, BF16),
            pltpu.VMEM(w_proj.shape, BF16),
            pltpu.VMEM((n, caps, width), BF16),
            pltpu.VMEM((n, caps, width), BF16),
            pltpu.VMEM((1, pairs), F32),
            pltpu.VMEM((1, pairs), F32),
            dma((loads,)),
        ]
        + [dma((half,)) for _ in range(8)],
        compiler_params=pltpu.CompilerParams(
            collective_id=0, has_side_effects=True, vmem_limit_bytes=64000000
        ),
    )(captions, caption_layout, images, w_query, w_keyval, w_out, w_up, w_down, w_proj)


def solution(mesh):
    return jax.shard_map(
        body,
        mesh=mesh,
        in_specs=(P("dp", None, None), P(), P("dp", None), P(), P(), P(), P(), P(), P()),
        out_specs=(P("dp", None), P("dp", None)),
        check_vma=False,
    )
```

time: 242 us -> 67.4 us (0.28)
  the two profiles are of different devices: /device:TPU:0 before, /device:TPU:29 now
where the time goes in v1:
time: 67.4 us; the launch traced here: 67.2 us
  Pallas kernels  57.4 us (85%)
  local copies, waits for them, and re-layouts  9.12 us (14%)
    pallas_call x1, Pallas kernels, body(): pl.pallas_call(functools.partial(kernel, n), out_shape=(out, out), in_spe...  57.4 us
    unnamed x3, local copies, waits for them, and re-layouts  9.12 us

profile of v1, /device:TPU:29, one launch (start us, length us, event | category | flops | bytes accessed | tf_op | source)
XLA Modules:
  0.0 67.2 jit_solution(14986849321853221836)
XLA Ops:
  0.6 6.0 %copy.11.cap_hbm = bf16[32,77,768]{2,1,0:T(8,128)(2,1)} copy(bf16[32,77,768]{2,0,1:T(8,128)(2,1)} %param.9) | data formatting | bytes 7569408 | tf_op args[0]
  6.7 57.4 %shard_map.104 = (f32[32,768]{1,0:T(8,128)}, f32[32,768]{1,0:T(8,128)}) custom-call(bf16[32,77,768]{2,1,0:T(8,128)(2,1)} %copy.11.cap_hbm, s32[2,1024]{1,0:T(2,128)} %layout.1, bf16[32,768]{1,0:T(8,128)(2,1)} %images.1, bf16[768,768]{1,0:T(8,128)(2,1)} %wq_hbm.1, bf16[768,1536]{1,0:T(8,128)(2,1)} %wkv_hbm.1, bf16[768,768]{1,0:T(8,128)(2,1)} %wo_hbm.1, ...), custom_call_target="tpu_custom_call" | custom-call | tf_op jit(solution)/shard_map/pallas_call | solution.py:298
  64.1 1.5 %copy.14 = f32[32,768]{1,0:T(8,128)} copy(f32[32,768]{1,0:T(8,128)} %get-tuple-element.4) | data formatting | bytes 196608
  65.6 1.5 %copy.15 = f32[32,768]{1,0:T(8,128)} copy(f32[32,768]{1,0:T(8,128)} %get-tuple-element.5) | data formatting | bytes 196608

commit v2 on v1

--- a/solution.py
+++ b/solution.py
@@ -11,9 +11,9 @@
 LOGIT_SCALE = 100.0
 EPS_NORM = 1e-05
 EPS_UNIT = 1e-06
-GROUP = 8
+GROUP = 16
+CAP_CHUNKS = 11
 QUAD = 4
-LSE_BLOCK = 256
 FF_CHUNKS = 4
 MESH = pl.DeviceIdType.MESH
 F32 = jnp.float32
@@ -52,16 +52,15 @@
     n,
     cap_hbm, layout, images, wq_hbm, wkv_hbm, wo_hbm, wup_hbm, wdown_hbm, wproj_hbm,
     image_out, text_out,
-    cap, normed, x_last, qk, mix, wq, wkv, wo, wup, wdown, wproj,
-    gi, gt, row_lse, col_lse,
-    load_sem, i_send, i_recv, i_rsend, i_rrecv, t_send, t_recv, t_rsend, t_rrecv,
+    cap, normed, qk, mix, wq, wkv, wo, wup, wdown, wproj,
+    gi, gt, lse,
+    load_sem, l_send, l_recv, i_send, i_recv, i_rsend, i_rrecv, t_send, t_recv, t_rsend, t_rrecv,
 ):
     me = lax.axis_index("dp")
     half = n // 2
     partner = me + 1 - 2 * lax.rem(me, 2)
-    caps, ctx, width = cap.shape
+    ctx, caps, width = cap.shape
     groups = caps // GROUP
-    slot = normed.shape[0] // caps
     head_dim = width // HEADS
     ff = wup.shape[1]
     fc = ff // FF_CHUNKS
@@ -74,9 +73,10 @@
         loads.append(copy)
         return copy
 
+    cap_steps = ctx // CAP_CHUNKS
     cap_loads = [
-        load(cap_hbm.at[pl.ds(g * GROUP, GROUP)], cap.at[pl.ds(g * GROUP, GROUP)])
-        for g in range(groups)
+        load(cap_hbm.at[pl.ds(i * cap_steps, cap_steps)], cap.at[pl.ds(i * cap_steps, cap_steps)])
+        for i in range(CAP_CHUNKS)
     ]
     wq_load = load(wq_hbm, wq)
     wkv_load = load(wkv_hbm, wkv)
@@ -93,12 +93,11 @@
 
     def greet(k, carry):
         pl.semaphore_signal(
-            barrier, inc=1, device_id=(lax.rem(me + 2 * k, n),), device_id_type=MESH
+            barrier, inc=1, device_id=(lax.rem(me + k, n),), device_id_type=MESH
         )
         return carry
 
-    lax.fori_loop(1, half, greet, 0)
-    pl.semaphore_signal(barrier, inc=1, device_id=(partner,), device_id_type=MESH)
+    lax.fori_loop(1, n, greet, 0)
 
     def remote(buf, block, send, recv, target):
         return pltpu.make_async_remote_copy(
@@ -147,33 +146,24 @@
     image = images[...].astype(F32)
     image_unit = unit_rows(image).astype(BF16)
     gi[me] = image_unit
-    pl.semaphore_wait(barrier, half)
+    pl.semaphore_wait(barrier, n - 1)
     push(*i_set)
 
-    token = lax.broadcasted_iota(jnp.int32, (ctx, width), 0)
-    tail = (ctx // 16) * 16
-    for g in range(groups):
-        cap_loads[g].wait()
-
-        def norm_one(i, carry, g=g):
-            c = g * GROUP + i
-            x = cap[c].astype(F32)
-            length = layout[0, me * caps + c]
-            x_last[pl.ds(c, 1), :] = jnp.sum(
-                jnp.where(token == length - 1, x, 0.0), axis=0, keepdims=True
-            )
-            base = pl.multiple_of(c * slot, 16)
+    row = lax.broadcasted_iota(jnp.int32, (caps, 128), 0)
+    length_rows = jnp.zeros((caps, 128), jnp.int32)
+    for c in range(caps):
+        length_rows = jnp.where(row == c, layout[0, me * caps + c], length_rows)
+    length_rows = jnp.concatenate([length_rows] * (width // 128), axis=1)
+
+    last = jnp.zeros((caps, width), F32)
+    for i in range(CAP_CHUNKS):
+        cap_loads[i].wait()
+        for t in range(i * cap_steps, (i + 1) * cap_steps):
+            x = cap[t].astype(F32)
+            last = jnp.where(length_rows == t + 1, x, last)
             y = layer_norm(x).astype(BF16)
-            normed[pl.ds(base, tail), :] = y[:tail]
-            rest = jnp.concatenate(
-                [y[tail:].astype(F32), jnp.zeros((slot - ctx, width), F32)], axis=0
-            )
-            normed[pl.ds(pl.multiple_of(base + tail, 16), slot - tail), :] = rest.astype(BF16)
-            return carry
-
-        lax.fori_loop(0, GROUP, norm_one, 0)
-
-    last = x_last[...]
+            for g in range(groups):
+                normed[g, t] = y[g * GROUP : (g + 1) * GROUP]
     last_normed = layer_norm(last).astype(BF16)
     wq_load.wait()
     query = dot(last_normed, wq[...]).astype(BF16).astype(F32) * (head_dim ** -0.5)
@@ -194,26 +184,22 @@
 
     cols = HEADS * GROUP
     col_cap = lax.rem(lax.broadcasted_iota(jnp.int32, (1, cols), 1), GROUP)
-
-    def attend(g, carry):
-        base = pl.multiple_of(g * (GROUP * slot), 16)
-        rows = normed[pl.ds(base, GROUP * slot), :]
-        first = pl.multiple_of(g * GROUP, GROUP)
-        keys = qk[:, pl.ds(first, GROUP), :].reshape(cols, width).astype(BF16)
+    row_index = lax.broadcasted_iota(jnp.int32, (ctx * GROUP, cols), 0)
+    same = lax.rem(row_index, GROUP) == col_cap
+
+    for g in range(groups):
+        rows = normed[g].reshape(ctx * GROUP, width)
+        keys = qk[:, g * GROUP : (g + 1) * GROUP, :].reshape(cols, width).astype(BF16)
         scores = dot_last(rows, keys)
         lengths = jnp.zeros((1, cols), jnp.int32)
         for i in range(GROUP):
             lengths = jnp.where(col_cap == i, layout[0, me * caps + g * GROUP + i], lengths)
-        place = lax.broadcasted_iota(jnp.int32, scores.shape, 0) - col_cap * slot
-        inside = (place >= 0) & (place < lengths)
+        inside = same & (row_index < lengths * GROUP)
         scores = jnp.where(inside, scores, -1e30)
         peak = jnp.max(scores, axis=0, keepdims=True)
         expo = jnp.where(inside, jnp.exp(scores - peak), 0.0)
         attn = (expo / jnp.sum(expo, axis=0, keepdims=True)).astype(BF16)
-        mix[:, pl.ds(first, GROUP), :] = dot_first(attn, rows).reshape(HEADS, GROUP, width)
-        return carry
-
-    lax.fori_loop(0, groups, attend, 0)
+        mix[:, g * GROUP : (g + 1) * GROUP, :] = dot_first(attn, rows).reshape(HEADS, GROUP, width)
 
     pieces = []
     for b in range(HEADS // QUAD):
@@ -245,51 +231,77 @@
     gt[me] = text_unit
     push(*t_set)
     finish(*i_set)
+
+    pairs = gi.shape[0] * gi.shape[1]
+    per_row = 128 // caps
+    spot = lax.broadcasted_iota(jnp.int32, (caps, 128), 1) - lax.rem(me, per_row) * caps
+    here = spot == row
+
+    def score(mine, others):
+        s = LOGIT_SCALE * dot_last(mine, others[...].reshape(pairs, width))
+        peak = jnp.max(s, axis=1, keepdims=True)
+        own = peak + jnp.log(jnp.sum(jnp.exp(s - peak), axis=1, keepdims=True))
+        return s, own
+
+    def pull(s, logsum, others):
+        weights = jnp.exp(s - logsum).astype(BF16)
+        return dot(weights, others[...].reshape(pairs, width))
+
+    def as_lanes(own):
+        return jnp.sum(jnp.where(here, own, 0.0), axis=0, keepdims=True)
+
+    text_scores, col_own = score(text_unit, gi)
+    text_pull = pull(text_scores, col_own, gi)
     relay(*t_set)
     finish(*t_set)
-
-    pairs = gi.shape[0] * gi.shape[1]
-    step_blocks = LSE_BLOCK // caps
-
-    def lse_block(b, carry):
-        where = pl.ds(pl.multiple_of(b * LSE_BLOCK, LSE_BLOCK), LSE_BLOCK)
-        for big, small, out in ((gi, gt, col_lse), (gt, gi, row_lse)):
-            all_rows = big[...].reshape(pairs, width)
-            block = small[pl.ds(b * step_blocks, step_blocks)].reshape(LSE_BLOCK, width)
-            s = LOGIT_SCALE * dot_last(all_rows, block)
-            peak = jnp.max(s, axis=0, keepdims=True)
-            out[:, where] = peak + jnp.log(jnp.sum(jnp.exp(s - peak), axis=0, keepdims=True))
+    image_scores, row_own = score(image_unit, gt)
+    lse[me] = jnp.concatenate([as_lanes(row_own), as_lanes(col_own)], axis=0)
+
+    def lse_copy(k, block, target):
+        return pltpu.make_async_remote_copy(
+            src_ref=lse.at[block], dst_ref=lse.at[block], send_sem=l_send.at[k],
+            recv_sem=l_recv.at[k], device_id=(target,), device_id_type=MESH,
+        )
+
+    def lse_send(k, carry):
+        lse_copy(k, me, lax.rem(me + k, n)).start()
         return carry
 
-    lax.fori_loop(0, pairs // LSE_BLOCK, lse_block, 0)
-
-    half_scale = 0.5 * LOGIT_SCALE
-
-    def grads(mine, others, other_lse, opposite):
-        every = others[...].reshape(pairs, width)
-        s = LOGIT_SCALE * dot_last(mine, every)
-        peak = jnp.max(s, axis=1, keepdims=True)
-        own = peak + jnp.log(jnp.sum(jnp.exp(s - peak), axis=1, keepdims=True))
-        weights = jnp.concatenate(
-            [jnp.exp(s - own), jnp.exp(s - other_lse)], axis=0
-        ).astype(BF16)
-        both = dot(weights, every)
-        total = both[:caps] + both[caps:]
-        return half_scale * total - LOGIT_SCALE * opposite.astype(F32)
-
-    image_out[...] = unit_back(image, grads(image_unit, gt, col_lse[...], text_unit))
-    text_out[...] = unit_back(text, grads(text_unit, gi, row_lse[...], image_unit))
+    def lse_wait(k, carry):
+        lse_copy(k, lax.rem(me + n - k, n), partner).wait_recv()
+        return carry
+
+    def lse_drain(k, carry):
+        lse_copy(k, me, partner).wait_send()
+        return carry
+
+    lax.fori_loop(1, n, lse_send, 0)
+    image_pull = pull(image_scores, row_own, gt)
+    lax.fori_loop(1, n, lse_wait, 0)
+    rows_cols = [
+        sum(lse[d] for d in range(start, start + per_row)) for start in range(0, n, per_row)
+    ]
+    every = jnp.concatenate(rows_cols, axis=1)
+    image_pull = image_pull + pull(image_scores, every[1:2], gt)
+    text_pull = text_pull + pull(text_scores, every[0:1], gi)
+
+    def finish_grad(x, total, opposite):
+        g = 0.5 * LOGIT_SCALE * total - LOGIT_SCALE * opposite.astype(F32)
+        return unit_back(x, g)
+
+    image_out[...] = finish_grad(image, image_pull, text_unit)
+    text_out[...] = finish_grad(text, text_pull, image_unit)
+    lax.fori_loop(1, n, lse_drain, 0)
     drain(*i_set)
     drain(*t_set)
 
 
 def body(captions, caption_layout, images, w_query, w_keyval, w_out, w_up, w_down, w_proj):
-    caps, ctx, width = captions.shape
+    captions = jnp.swapaxes(captions, 0, 1)
+    ctx, caps, width = captions.shape
     n = lax.axis_size("dp")
-    slot = -(-ctx // 16) * 16
     half = n // 2
-    pairs = n * caps
-    loads = caps // GROUP + 4 + 2 * FF_CHUNKS
+    loads = CAP_CHUNKS + 4 + 2 * FF_CHUNKS
     any_spec = pl.BlockSpec(memory_space=pl.ANY)
     vmem = pl.BlockSpec(memory_space=pltpu.VMEM)
     smem = pl.BlockSpec(memory_space=pltpu.SMEM)
@@ -302,8 +314,7 @@
         out_specs=(vmem, vmem),
         scratch_shapes=[
             pltpu.VMEM(captions.shape, BF16),
-            pltpu.VMEM((caps * slot, width), BF16),
-            pltpu.VMEM((caps, width), F32),
+            pltpu.VMEM((caps // GROUP, ctx, GROUP, width), BF16),
             pltpu.VMEM((HEADS, caps, width), F32),
             pltpu.VMEM((HEADS, caps, width), F32),
             pltpu.VMEM(w_query.shape, BF16),
@@ -314,9 +325,10 @@
             pltpu.VMEM(w_proj.shape, BF16),
             pltpu.VMEM((n, caps, width), BF16),
             pltpu.VMEM((n, caps, width), BF16),
-            pltpu.VMEM((1, pairs), F32),
-            pltpu.VMEM((1, pairs), F32),
+            pltpu.VMEM((n, 2, 128), F32),
             dma((loads,)),
+            dma((n,)),
+            dma((n,)),
         ]
         + [dma((half,)) for _ in range(8)],
         compiler_params=pltpu.CompilerParams(

time: 67.4 us -> 65.1 us (0.966)
  the two profiles are of different devices: /device:TPU:29 before, /device:TPU:0 now
where the time goes in v2:
time: 65.1 us; the launch traced here: 64.9 us
  Pallas kernels  61.1 us (94%)
  local copies, waits for them, and re-layouts  3.08 us (5%)
    pallas_call x1, Pallas kernels, body(): pl.pallas_call(functools.partial(kernel, n), out_shape=(out, out), in_spe...  61.1 us
    unnamed x2, local copies, waits for them, and re-layouts  3.08 us

profile of v2, /device:TPU:0, one launch (start us, length us, event | category | flops | bytes accessed | tf_op | source)
XLA Modules:
  0.0 64.9 jit_solution(11108560720225661923)
XLA Ops:
  0.6 61.1 %shard_map.104 = (f32[32,768]{1,0:T(8,128)}, f32[32,768]{1,0:T(8,128)}) custom-call(bf16[77,32,768]{2,1,0:T(8,128)(2,1)} %bitcast.1, s32[2,1024]{1,0:T(2,128)} %layout.1, bf16[32,768]{1,0:T(8,128)(2,1)} %images.1, bf16[768,768]{1,0:T(8,128)(2,1)} %wq_hbm.1, bf16[768,1536]{1,0:T(8,128)(2,1)} %wkv_hbm.1, bf16[768,768]{1,0:T(8,128)(2,1)} %wo_hbm.1, ...), custom_call_target="tpu_custom_call" | custom-call | tf_op jit(solution)/shard_map/pallas_call | solution.py:310
  61.8 1.5 %copy.13 = f32[32,768]{1,0:T(8,128)} copy(f32[32,768]{1,0:T(8,128)} %get-tuple-element.4) | data formatting | bytes 196608
  63.3 1.5 %copy.14 = f32[32,768]{1,0:T(8,128)} copy(f32[32,768]{1,0:T(8,128)} %get-tuple-element.5) | data formatting | bytes 196608

commit v3 on v2

--- a/solution.py
+++ b/solution.py
@@ -105,40 +105,92 @@
             device_id=(target,), device_id_type=MESH,
         )
 
+    depth = n // 8
+    side = me + 2 - 4 * lax.rem(me // 2, 2)
+    over = me + 4 - 8 * lax.rem(me // 4, 2)
+    across = side + over - me
+    upper = (0, caps // 2)
+    lower = (caps // 2, caps // 2)
+
+    def shift(base, k):
+        return lax.rem(base + n - 8 * k, n)
+
+    def move(buf, block, send, recv, index, target, part):
+        ref = buf.at[block, pl.ds(*part)]
+        return pltpu.make_async_remote_copy(
+            src_ref=ref, dst_ref=ref, send_sem=send.at[index], recv_sem=recv.at[index],
+            device_id=(target,), device_id_type=MESH,
+        )
+
     def push(buf, send, recv, rsend, rrecv):
         def step(k, carry):
-            remote(buf, me, send.at[k], recv.at[k], lax.rem(me + 2 * k, n)).start()
-            return carry
-
-        lax.fori_loop(1, half, step, 0)
+            remote(buf, me, send.at[k], recv.at[k], lax.rem(me + 8 * k, n)).start()
+            return carry
+
+        remote(buf, me, send.at[depth], recv.at[depth], side).start()
+        remote(buf, me, send.at[2 * depth], recv.at[2 * depth], over).start()
+        lax.fori_loop(1, depth, step, 0)
         remote(buf, me, rsend.at[0], rrecv.at[0], partner).start()
 
     def relay(buf, send, recv, rsend, rrecv):
-        def step(k, carry):
-            block = lax.rem(me + n - 2 * k, n)
+        def first(k, carry):
+            block = shift(me, k)
             remote(buf, block, send.at[k], recv.at[k], partner).wait_recv()
+            remote(buf, block, send.at[depth + k], recv.at[depth + k], side).start()
+            remote(buf, block, send.at[2 * depth + k], recv.at[2 * depth + k], over).start()
             remote(buf, block, rsend.at[k], rrecv.at[k], partner).start()
             return carry
 
-        lax.fori_loop(1, half, step, 0)
+        def second(k, carry):
+            for kind, base, target, part in ((1, side, over, upper), (2, over, side, lower)):
+                block = shift(base, k)
+                place = kind * depth + k
+                remote(buf, block, send.at[place], recv.at[place], partner).wait_recv()
+                move(buf, block, send, recv, (kind + 2) * depth + k, target, part).start()
+                remote(buf, block, rsend.at[place], rrecv.at[place], partner).start()
+            return carry
+
+        def third(k, carry):
+            block = shift(across, k)
+            move(buf, block, send, recv, 3 * depth + k, partner, upper).wait_recv()
+            move(buf, block, send, recv, 4 * depth + k, partner, lower).wait_recv()
+            place = 3 * depth + k
+            remote(buf, block, rsend.at[place], rrecv.at[place], partner).start()
+            return carry
+
+        lax.fori_loop(1, depth, first, 0)
+        lax.fori_loop(0, depth, second, 0)
+        lax.fori_loop(0, depth, third, 0)
 
     def finish(buf, send, recv, rsend, rrecv):
         def step(k, carry):
-            block = lax.rem(partner + n - 2 * k, n)
-            remote(buf, block, rsend.at[k], rrecv.at[k], partner).wait_recv()
-            return carry
-
-        lax.fori_loop(0, half, step, 0)
+            for kind, base in enumerate((me, side, over, across)):
+                block = shift(base + partner - me, k)
+                place = kind * depth + k
+                remote(buf, block, rsend.at[place], rrecv.at[place], partner).wait_recv()
+            return carry
+
+        lax.fori_loop(0, depth, step, 0)
 
     def drain(buf, send, recv, rsend, rrecv):
         def step(k, carry):
-            block = lax.rem(me + n - 2 * k, n)
+            for kind, base in enumerate((me, side, over, across)):
+                block = shift(base, k)
+                place = kind * depth + k
+                remote(buf, block, rsend.at[place], rrecv.at[place], partner).wait_send()
+            for kind in (1, 2):
+                place = kind * depth + k
+                remote(buf, me, send.at[place], recv.at[place], partner).wait_send()
+            move(buf, me, send, recv, 3 * depth + k, partner, upper).wait_send()
+            move(buf, me, send, recv, 4 * depth + k, partner, lower).wait_send()
+            return carry
+
+        def near(k, carry):
             remote(buf, me, send.at[k], recv.at[k], partner).wait_send()
-            remote(buf, block, rsend.at[k], rrecv.at[k], partner).wait_send()
-            return carry
-
-        lax.fori_loop(1, half, step, 0)
-        remote(buf, me, rsend.at[0], rrecv.at[0], partner).wait_send()
+            return carry
+
+        lax.fori_loop(1, depth, near, 0)
+        lax.fori_loop(0, depth, step, 0)
 
     i_set = (gi, i_send, i_recv, i_rsend, i_rrecv)
     t_set = (gt, t_send, t_recv, t_rsend, t_rrecv)
@@ -330,7 +382,7 @@
             dma((n,)),
             dma((n,)),
         ]
-        + [dma((half,)) for _ in range(8)],
+        + [dma((count,)) for count in (5 * n // 8, 5 * n // 8, half, half) * 2],
         compiler_params=pltpu.CompilerParams(
             collective_id=0, has_side_effects=True, vmem_limit_bytes=64000000
         ),

time: 65.1 us -> 53.7 us (0.82)
  Pallas kernels: 61.1 us -> 49.7 us
    pallas_call x1, Pallas kernels: 61.1 us -> 49.7 us  [body(): pl.pallas_call(functools.partial(kernel, n), out_shape=(out, out), in_spe...]
where the time goes in v3:
time: 53.7 us; the launch traced here: 53.4 us
  Pallas kernels  49.7 us (93%)
  local copies, waits for them, and re-layouts  3.08 us (6%)
  between operations  0.64 us (1%)
    pallas_call x1, Pallas kernels, body(): pl.pallas_call(functools.partial(kernel, n), out_shape=(out, out), in_spe...  49.7 us
    unnamed x2, local copies, waits for them, and re-layouts  3.08 us

profile of v3, /device:TPU:0, one launch (start us, length us, event | category | flops | bytes accessed | tf_op | source)
XLA Modules:
  0.0 53.4 jit_solution(10628395644797416526)
XLA Ops:
  0.6 49.7 %shard_map.104 = (f32[32,768]{1,0:T(8,128)}, f32[32,768]{1,0:T(8,128)}) custom-call(bf16[77,32,768]{2,1,0:T(8,128)(2,1)} %bitcast.1, s32[2,1024]{1,0:T(2,128)} %layout.1, bf16[32,768]{1,0:T(8,128)(2,1)} %images.1, bf16[768,768]{1,0:T(8,128)(2,1)} %wq_hbm.1, bf16[768,1536]{1,0:T(8,128)(2,1)} %wkv_hbm.1, bf16[768,768]{1,0:T(8,128)(2,1)} %wo_hbm.1, ...), custom_call_target="tpu_custom_call" | custom-call | tf_op jit(solution)/shard_map/pallas_call | solution.py:362
  50.4 1.5 %copy.13 = f32[32,768]{1,0:T(8,128)} copy(f32[32,768]{1,0:T(8,128)} %get-tuple-element.4) | data formatting | bytes 196608
  51.9 1.5 %copy.14 = f32[32,768]{1,0:T(8,128)} copy(f32[32,768]{1,0:T(8,128)} %get-tuple-element.5) | data formatting | bytes 196608
